TPU v7x, 32 devices: a whole 2x2x4 slice. The times are simulated.
32 devices in a mesh: tm: 16 (over z, x, core), chan: 2 (over y).
Axes of the slice: x: 2, y: 2, z: 4, core: 2. Of those that a mesh axis runs over, the one named last changes fastest.
Arguments:
- trans: float32 [4, 128, 32768], P(None, 'chan', 'tm'), may hold values from -1 to 1
- drive: float32 [2, 128, 32768], P(None, 'chan', 'tm'), may hold values from -60 to 60
- back_drive: float32 [2, 128, 32768], P(None, 'chan', 'tm'), may hold values from -60 to 60
- readout: float32 [128, 2, 128], P('chan'), may hold values from -0.375 to 0.375
Outputs:
- observed: float32 [128, 32768], P('chan', 'tm')
All inputs are finite; a program needn't handle non-finite values.
Results may differ from a plain program's by a relative error of at most 0.0003.
Values sent between devices are 32-bit elements; how exact they have to be, the bound alone decides.
A program may use at most 64 MiB of HBM per device.

v0:
```python
import jax
import jax.numpy as jnp
from jax import lax
from jax.sharding import PartitionSpec as P

epsilon = 1e-06
identity_fill = (1.0, 0.0, 0.0, 1.0, 0.0, 0.0)


def prefix(part, axis, combine, identity, reverse):
    count = lax.axis_size(axis)
    place = lax.axis_index(axis)
    ahead = count - 1 - place if reverse else place
    gathered = jax.tree.map(lambda a: lax.all_gather(a, axis), part)
    state = jax.tree.map(lambda a, e: jnp.zeros_like(a) + jnp.asarray(e, a.dtype), part, identity)

    def one(hop, state):
        source = count - 1 - hop if reverse else hop
        return combine(
            state, jax.tree.map(lambda a: lax.dynamic_index_in_dim(a, source, 0, False), gathered)
        )

    return lax.fori_loop(0, ahead, one, state)


def compose(earlier, later):
    return (
        later[0] * earlier[0] + later[1] * earlier[2],
        later[0] * earlier[1] + later[1] * earlier[3],
        later[2] * earlier[0] + later[3] * earlier[2],
        later[2] * earlier[1] + later[3] * earlier[3],
        later[0] * earlier[4] + later[1] * earlier[5] + later[4],
        later[2] * earlier[4] + later[3] * earlier[5] + later[5],
    )


def shifted_part(array, offset, fill_value, reverse):
    filler = jnp.full((array.shape[0], offset), fill_value, array.dtype)
    if reverse:
        return jnp.concatenate([array[:, offset:], filler], axis=1)
    return jnp.concatenate([filler, array[:, :-offset]], axis=1)


def doubling_scan(pieces, reverse):
    length = pieces[0].shape[1]
    offset = 1
    while offset < length:
        shifted = tuple(
            (
                shifted_part(piece, offset, fill_value, reverse)
                for piece, fill_value in zip(pieces, identity_fill)
            )
        )
        pieces = compose(shifted, pieces)
        offset = offset * 2
    return pieces


def apply_carry(maps, carry):
    first = carry[0][:, None]
    second = carry[1][:, None]
    return (
        maps[0] * first + maps[1] * second + maps[4],
        maps[2] * first + maps[3] * second + maps[5],
    )


def on_device(trans, drive, back_drive, readout):
    channels = trans.shape[1]
    steps = trans.shape[2]
    devices_tm = lax.axis_size("tm")
    forward = doubling_scan((trans[0], trans[1], trans[2], trans[3], drive[0], drive[1]), False)
    backward = doubling_scan(
        (trans[0], trans[2], trans[1], trans[3], back_drive[0], back_drive[1]), True
    )
    ones = jnp.ones((channels,), jnp.float32)
    zeros = jnp.zeros((channels,), jnp.float32)
    identity = (ones, zeros, zeros, ones, zeros, zeros)
    before = prefix(
        (
            forward[0][:, -1],
            forward[1][:, -1],
            forward[2][:, -1],
            forward[3][:, -1],
            forward[4][:, -1],
            forward[5][:, -1],
        ),
        "tm",
        compose,
        identity,
        False,
    )
    after = prefix(
        (
            backward[0][:, 0],
            backward[1][:, 0],
            backward[2][:, 0],
            backward[3][:, 0],
            backward[4][:, 0],
            backward[5][:, 0],
        ),
        "tm",
        compose,
        identity,
        True,
    )
    forward_states = apply_carry(forward, (before[4], before[5]))
    backward_states = apply_carry(backward, (after[4], after[5]))
    sum_f, sum_b = lax.psum(
        (
            jnp.sum(
                forward_states[0] * forward_states[0] + forward_states[1] * forward_states[1],
                axis=1,
            ),
            jnp.sum(
                backward_states[0] * backward_states[0] + backward_states[1] * backward_states[1],
                axis=1,
            ),
        ),
        "tm",
    )
    count = 2.0 * steps * devices_tm
    norm_f = jnp.sqrt(sum_f / count + epsilon)[:, None]
    norm_b = jnp.sqrt(sum_b / count + epsilon)[:, None]
    smoothed = jnp.stack(
        [
            forward_states[0] / norm_f + backward_states[0] / norm_b,
            forward_states[1] / norm_f + backward_states[1] / norm_b,
        ],
        axis=0,
    )
    full_readout = lax.all_gather(readout, "chan", axis=0, tiled=True)
    mine = lax.dynamic_slice_in_dim(full_readout, lax.axis_index("chan") * channels, channels, 2)
    flat = mine.reshape(mine.shape[0], -1)
    right = smoothed.reshape(-1, steps)
    observed = lax.psum_scatter(
        jnp.dot(flat, right, precision=lax.Precision.HIGHEST, preferred_element_type=jnp.float32),
        "chan",
        scatter_dimension=0,
        tiled=True,
    )
    return observed


def solution(mesh):
    in_specs = (
        P(None, "chan", "tm"),
        P(None, "chan", "tm"),
        P(None, "chan", "tm"),
        P("chan", None, None),
    )
    out_specs = P("chan", "tm")
    return jax.shard_map(
        on_device, mesh=mesh, in_specs=in_specs, out_specs=out_specs, check_vma=False
    )
```

profile of v0, /device:TPU:0, one launch (start us, length us, event | category | flops | bytes accessed | tf_op | source)
XLA Modules:
  0.0 184.8 jit_solution(10169155482427554681)
XLA Ops:
  6.5 1.4 slice_bitcast_fusion.1
  8.6 1.1 copy-done.1
  11.3 1.3 fusion.95
  12.6 1.3 fusion.97
  29.0 1.1 fusion.76
  30.1 1.0 fusion.72
  31.2 1.1 fusion.71
  32.3 1.1 fusion.78
  35.2 0.9 slice_reduce_fusion.3
  36.1 0.9 slice_reduce_fusion.2
  37.0 0.9 slice_reduce_fusion.1
  38.7 2.4 %add_add_fusion.32 = (f32[64,2048]{1,0:T(8,128)S(1)}, f32[64,2048]{1,0:T(8,128)S(1)}, f32[64,2048]{1,0:T(8,128)S(1)}, f32[64,2048]{1,0:T(8,128)S(1)}, f32[64,2048]{1,0:T(8,128)S(1)}, /*index=5*/f32[64,2048]{1,0:T(8,128)S(1)}) fusion(f32[64,2048]{1,0:T(8,128)S(1)} %get-tuple-element.505, f32[64,2046]{1,0:T(8,128)S(1)} %bitcast.215, ...), kind=kLoop, calls=%fused_computation.234 | loop fusion | flops 2621440 | bytes 9435136 | tf_op jit(solution)/shard_map/add | solution.py:33
  41.1 0.9 add_add_fusion.30
  42.0 0.9 add_add_fusion.28
  42.9 0.9 add_add_fusion.26
  43.8 0.9 add_add_fusion.24
  44.7 0.9 add_add_fusion.22
  45.7 0.9 add_add_fusion.20
  55.2 63.1 %all-reduce.145 = (f32[1024]{0:T(1024)S(1)}, f32[1024]{0:T(1024)S(1)}, f32[1024]{0:T(1024)S(1)}, f32[1024]{0:T(1024)S(1)}, f32[1024]{0:T(1024)S(1)}, /*index=5*/...) all-reduce(f32[1024]{0:T(1024)S(1)} %dynamic-update-slice.6, ...), channel_id=8, replica_groups=mesh['tm'=16,'chan'=2] {'tm'}, use_global_device_ids=true, to_apply=%add.138 | all-reduce | flops 12288 | bytes 98304
  119.9 2.7 %add_reduce_fusion = (f32[64]{0:T(128)S(1)}, f32[64,2048]{1,0:T(8,128)}, f32[64,2048]{1,0:T(8,128)}) fusion(f32[64,2048]{1,0:T(8,128)S(1)} %copy-done.3, f32[64,2048]{1,0:T(8,128)} %get-tuple-element.554, f32[64]{0:T(128)S(1)} %get-tuple-element.327, f32[64,2048]{1,0:T(8,128)} %get-tuple-element.553, f32[64]{0:T(128)S(1)} %get-tuple-element.326, ...), kind=kLoop, calls=%fused_computation.166 | loop fusion | flops 1572800 | bytes 4195072 | tf_op jit(solution)/shard_map/reduce_sum | solution.py:115
  123.2 29.5 %all-reduce.144 = (f32[64]{0:T(128)S(1)}, f32[64]{0:T(128)S(1)}) all-reduce(f32[64]{0:T(128)S(1)} %get-tuple-element.385, f32[64]{0:T(128)S(1)} %get-tuple-element.382), channel_id=1, replica_groups=mesh['tm'=16,'chan'=2] {'tm'}, use_global_device_ids=true, to_apply=%region_7.8 | all-reduce | flops 128 | bytes 1024 | tf_op jit(solution)/shard_map/psum | solution.py:109
  152.7 4.9 %all_gather.39 = f32[128,2,128]{2,1,0:T(2,128)S(1)} all-gather(f32[64,2,128]{2,1,0:T(2,128)S(1)} %copy-done.17), channel_id=1, replica_groups=mesh['tm'=16,'chan'=2] {'chan'}, dimensions={0}, use_global_device_ids=true | all-gather | bytes 196608 | tf_op jit(solution)/shard_map/all_gather | solution.py:132
  158.0 2.0 %convolution_bitcast_fusion = f32[128,2048]{1,0:T(8,128)} fusion(f32[1,64,2048]{2,1,0:T(8,128)S(1)} %get-tuple-element.566, f32[1,64,2048]{2,1,0:T(8,128)S(1)} %get-tuple-element.565, f32[128,2,64]{2,1,0:T(2,128)S(1)} %constant_dynamic-slice_fusion.12), kind=kOutput, calls=%fused_computation.40 | convolution fusion | flops 402915328 | bytes 2162688 | tf_op jit(solution)/shard_map/dot_general | solution.py:137
  160.1 17.8 %reduce-scatter.2.cloned.1.call-done = f32[64,2048]{1,0:T(8,128)} async-done(((f32[128,2048]{1,0:T(8,128)}), f32[64,2048]{1,0:T(8,128)}) %reduce-scatter.2.cloned.1.call-update) | async-done | bytes 524304 | tf_op jit(solution)/shard_map/reduce_scatter | solution.py:136
  (231 shorter events, 30.0 us)
Async XLA Ops:
  6.5 1.9 %copy-start = (f32[4,64,2048]{2,1,0:T(8,128)S(1)}, f32[4,64,2048]{2,1,0:T(8,128)}, u32[]{:S(2)}) copy-start(f32[4,64,2048]{2,1,0:T(8,128)} %param.8) | copy-start | bytes 6291460
  6.5 171.4 %reduce-scatter.2.cloned.1.call-start = ((), (), s32[]{:S(2)}) async-start(), calls=%async_computation.1 | async-start | bytes 1572864 | tf_op jit(solution)/shard_map/reduce_scatter | solution.py:136
  8.4 1.2 copy-start.1
  10.0 1.2 copy-start.2
  49.2 2.2 %copy-start.18 = (u32[32]{0:T(128)S(1)}, u32[32]{0:T(128)}, u32[]{:S(2)}) copy-start(u32[32]{0:T(128)} %constant.381) | copy-start | bytes 388
  49.2 70.7 %copy-start.3 = (f32[64,2048]{1,0:T(8,128)S(1)}, f32[64,2048]{1,0:T(8,128)}, u32[]{:S(2)}) copy-start(f32[64,2048]{1,0:T(8,128)} %get-tuple-element.448) | copy-start | bytes 1572868
  49.2 70.7 %copy-start.4 = (f32[64,2048]{1,0:T(8,128)S(1)}, f32[64,2048]{1,0:T(8,128)}, u32[]{:S(2)}) copy-start(f32[64,2048]{1,0:T(8,128)} %get-tuple-element.451) | copy-start | bytes 1572868
  49.2 70.7 %copy-start.5 = (f32[64,2048]{1,0:T(8,128)S(1)}, f32[64,2048]{1,0:T(8,128)}, u32[]{:S(2)}) copy-start(f32[64,2048]{1,0:T(8,128)} %get-tuple-element.551) | copy-start | bytes 1572868
  49.2 70.7 %copy-start.6 = (f32[64,2048]{1,0:T(8,128)S(1)}, f32[64,2048]{1,0:T(8,128)}, u32[]{:S(2)}) copy-start(f32[64,2048]{1,0:T(8,128)} %get-tuple-element.552) | copy-start | bytes 1572868
  49.5 0.8 copy-start.7
  49.5 1.1 copy-start.9
  49.5 1.3 copy-start.11
  49.5 1.5 copy-start.13
  119.9 2.8 %copy-start.8 = (f32[64,2048]{1,0:T(8,128)S(1)}, f32[64,2048]{1,0:T(8,128)}, u32[]{:S(2)}) copy-start(f32[64,2048]{1,0:T(8,128)} %copy-done.7) | copy-start | bytes 1572868
  119.9 2.8 %copy-start.10 = (f32[64,2048]{1,0:T(8,128)S(1)}, f32[64,2048]{1,0:T(8,128)}, u32[]{:S(2)}) copy-start(f32[64,2048]{1,0:T(8,128)} %copy-done.9) | copy-start | bytes 1572868
  119.9 2.8 %copy-start.12 = (f32[64,2048]{1,0:T(8,128)S(1)}, f32[64,2048]{1,0:T(8,128)}, u32[]{:S(2)}) copy-start(f32[64,2048]{1,0:T(8,128)} %copy-done.11) | copy-start | bytes 1572868
  119.9 2.8 %copy-start.14 = (f32[64,2048]{1,0:T(8,128)S(1)}, f32[64,2048]{1,0:T(8,128)}, u32[]{:S(2)}) copy-start(f32[64,2048]{1,0:T(8,128)} %copy-done.13) | copy-start | bytes 1572868
  122.7 30.0 %copy-start.17 = (f32[64,2,128]{2,1,0:T(2,128)S(1)}, f32[64,2,128]{2,1,0:T(2,128)}, u32[]{:S(2)}) copy-start(f32[64,2,128]{2,1,0:T(2,128)} %param.11) | copy-start | bytes 196612
  122.7 35.2 %copy-start.15 = (f32[64,2048]{1,0:T(8,128)S(1)}, f32[64,2048]{1,0:T(8,128)}, u32[]{:S(2)}) copy-start(f32[64,2048]{1,0:T(8,128)} %get-tuple-element.386) | copy-start | bytes 1572868
  122.7 35.1 %copy-start.16 = (f32[64,2048]{1,0:T(8,128)S(1)}, f32[64,2048]{1,0:T(8,128)}, u32[]{:S(2)}) copy-start(f32[64,2048]{1,0:T(8,128)} %get-tuple-element.387) | copy-start | bytes 1572868
Sparse Core Ops, SparseCore 0:
  160.2 17.6 reduce-scatter.1
where the time goes:
time: 185 us
  blocking collectives  97.5 us (53%)
  local copies, waits for them, and re-layouts  26.6 us (14%)
  other arithmetic  25.4 us (14%)
  waiting for transfers between devices  17.8 us (10%)
  between operations  15 us (8%)
  matrix products  2.04 us (1%)
    unnamed x1, blocking collectives  63.1 us
    psum x1, blocking collectives, on_device(): lax.psum((jnp.sum(forward_states[0] * forward_states[0] + forward_states[...  29.5 us
    reduce_scatter x1, waiting for transfers between devices, on_device(): lax.psum_scatter(jnp.dot(flat, right, precision=lax.Precision.HIGHEST, pr...  17.8 us
    add x37, other arithmetic, compose(): later[2] * earlier[4] + later[3] * earlier[5] + later[5]  13.1 us
    slice x62, local copies, waits for them, and re-layouts, shifted_part(): return jnp.concatenate([array[:, offset:], filler], axis=1)  8.38 us
    unnamed x63, local copies, waits for them, and re-layouts  5.75 us
    all_gather x1, blocking collectives, on_device(): full_readout = lax.all_gather(readout, 'chan', axis=0, tiled=True)  4.93 us
    add x10, other arithmetic, compose(): later[0] * earlier[4] + later[1] * earlier[5] + later[4]  4.51 us
  transfers between devices with their start and end apart: 1, of which 1 were waited for; matrix products, arithmetic and copies ran while one was open for 0% of the time, Pallas kernels for 0%

commit v1 on v0

v1 whole, which is shorter than its diff:
```python
import functools

import jax
import jax.numpy as jnp
from jax import lax
from jax.experimental import pallas as pl
from jax.experimental.pallas import tpu as pltpu
from jax.sharding import PartitionSpec as P

MESH = pl.DeviceIdType.MESH
epsilon = 1e-06
LANES = 128
ROWS = 8


def cmul(ar, ai, br, bi):
    return ar * br - ai * bi, ar * bi + ai * br


def lane_total(value, width):
    shift = width
    while shift < LANES:
        value = value + pltpu.roll(value, shift, 1)
        shift *= 2
    return value


def chunk_prefix(maps, width, reverse):
    zr, zi, fr, fi = maps
    one = jnp.ones((1, LANES), jnp.float32)
    nil = jnp.zeros((1, LANES), jnp.float32)
    state = (one, nil, nil, nil)
    ahead = [None] * ROWS
    for k in range(ROWS - 1, -1, -1) if reverse else range(ROWS):
        ahead[k] = state
        pr, pi, ur, ui = state
        kr, ki = zr[k : k + 1], zi[k : k + 1]
        pr, pi = cmul(kr, ki, pr, pi)
        ur, ui = cmul(kr, ki, ur, ui)
        state = (pr, pi, ur + fr[k : k + 1], ui + fi[k : k + 1])
    rows = [jnp.concatenate([a[i] for a in ahead], axis=0) for i in range(4)]
    total = [jnp.broadcast_to(a, (ROWS, LANES)) for a in state]
    lane = lax.broadcasted_iota(jnp.int32, (ROWS, LANES), 1)
    if reverse:
        shift, edge, last = LANES - width, lane >= LANES - width, lane < width
    else:
        shift, edge, last = width, lane < width, lane >= LANES - width
    blocks = LANES // width

    def exclusive(inc):
        if blocks == 1:
            return [jnp.full((ROWS, LANES), e, jnp.float32) for e in (1.0, 0.0, 0.0, 0.0)]
        return [
            jnp.where(edge, e, pltpu.roll(a, shift, 1)) for a, e in zip(inc, (1.0, 0.0, 0.0, 0.0))
        ]

    inc = total
    for _ in range(blocks - 1):
        er, ei, gr, gi = exclusive(inc)
        er, ei = cmul(total[0], total[1], er, ei)
        gr, gi = cmul(total[0], total[1], gr, gi)
        inc = [er, ei, gr + total[2], gi + total[3]]
    er, ei, gr, gi = exclusive(inc)
    pr, pi = cmul(rows[0], rows[1], er, ei)
    ur, ui = cmul(rows[0], rows[1], gr, gi)
    whole = [lane_total(jnp.where(last, a, 0.0), width) for a in inc]
    return (pr, pi, ur + rows[2], ui + rows[3]), whole


def device_row(ahead, whole, sums, width):
    pr, pi, ur, ui = ahead
    s0, s1r, s1i, s2 = sums
    d0 = s0 + 2.0 * (ur * s1r + ui * s1i) + (ur * ur + ui * ui) * s2
    d1r, d1i = cmul(pr, -pi, s1r + ur * s2, s1i + ui * s2)
    d2 = (pr * pr + pi * pi) * s2
    sums = [jnp.sum(a, axis=0, keepdims=True) for a in (d0, d1r, d1i, d2)]
    sums = lane_total(jnp.concatenate(sums + sums, axis=0), width)
    return jnp.concatenate([a[0:1] for a in whole] + [sums[0:4]], axis=0)


def split(value):
    high = value.astype(jnp.bfloat16)
    return high, (value - high.astype(jnp.float32)).astype(jnp.bfloat16)


def body(
    n_tm,
    n_ch,
    trans,
    drive,
    back,
    readout,
    out,
    raw,
    turned,
    scans,
    smooth,
    reads,
    weights,
    gath,
    sends,
    recvs,
    own,
    final,
    in_sem,
    read_in,
    read_send,
    read_recv,
    gath_send,
    gath_recv,
    part_send,
    part_recv,
    out_sem,
):
    width = trans.shape[1]
    steps = trans.shape[2]
    blocks = LANES // width
    span = steps // blocks
    length = span // ROWS
    pitch = length + ROWS
    tiles = span // LANES
    outs = readout.shape[0] // 2
    me = lax.axis_index("tm")
    group = lax.axis_index("chan")

    planes = (trans.at[0], trans.at[2], drive.at[0], drive.at[1], back.at[0], back.at[1])
    loads = [pltpu.make_async_copy(src, raw.at[i], in_sem.at[i]) for i, src in enumerate(planes)]
    for copy in loads:
        copy.start()
    read_copy = pltpu.make_async_copy(readout, reads.at[0], read_in)
    read_copy.start()

    barrier = pltpu.get_barrier_semaphore()
    for d in range(1, n_tm):
        pl.semaphore_signal(
            barrier, inc=1, device_id={"tm": lax.rem(me + d, n_tm)}, device_id_type=MESH
        )
    for d in range(1, n_ch):
        pl.semaphore_signal(
            barrier, inc=1, device_id={"chan": lax.rem(group + d, n_ch)}, device_id_type=MESH
        )

    for i, copy in enumerate(loads):
        copy.wait()
        for b in range(tiles):
            block = jnp.concatenate(
                [
                    raw[i, :, h * span + b * LANES : h * span + (b + 1) * LANES]
                    for h in range(blocks)
                ],
                axis=0,
            ).T
            for at in range(0, LANES, length):
                k = (b * LANES + at) // length
                turned[i, k * pitch : k * pitch + length, :] = block[at : at + length]

    read_copy.wait()
    pl.semaphore_wait(barrier, n_tm + n_ch - 2)
    read_sends = []
    for d in range(1, n_ch):
        copy = pltpu.make_async_remote_copy(
            src_ref=reads.at[0],
            dst_ref=reads.at[d],
            send_sem=read_send.at[d],
            recv_sem=read_recv.at[d],
            device_id={"chan": lax.rem(group + d, n_ch)},
            device_id_type=MESH,
        )
        copy.start()
        read_sends.append(copy)

    nil = jnp.zeros((ROWS, LANES), jnp.float32)
    one = jnp.ones((ROWS, LANES), jnp.float32)

    def advance(state, p, q, dr, di):
        fr, fi, ar, ai, s0, s1r, s1i, s2 = state
        fr, fi = p * fr - q * fi + dr, q * fr + p * fi + di
        ar, ai = p * ar - q * ai, q * ar + p * ai
        s0 = s0 + (fr * fr + fi * fi)
        s1r = s1r + (ar * fr + ai * fi)
        s1i = s1i + (ar * fi - ai * fr)
        s2 = s2 + (ar * ar + ai * ai)
        return fr, fi, ar, ai, s0, s1r, s1i, s2

    def scan_step(s, state):
        f, g = state
        rows = pl.ds(s, ROWS, stride=pitch)
        f = advance(
            f,
            turned.at[0][rows, :],
            turned.at[1][rows, :],
            turned.at[2][rows, :],
            turned.at[3][rows, :],
        )
        r = length - 1 - s
        rows = pl.ds(r, ROWS, stride=pitch)
        g = advance(
            g,
            turned.at[0][rows, :],
            -turned.at[1][rows, :],
            turned.at[4][rows, :],
            turned.at[5][rows, :],
        )
        for i in range(4):
            scans[i, s] = f[i]
            scans[4 + i, r] = g[i]
        return f, g

    start = (nil, nil, one, nil, nil, nil, nil, nil)
    f, g = lax.fori_loop(0, length, scan_step, (start, start), unroll=4)
    ahead_f, whole_f = chunk_prefix((f[2], f[3], f[0], f[1]), width, False)
    ahead_b, whole_b = chunk_prefix((g[2], g[3], g[0], g[1]), width, True)
    gath[0, 0:ROWS] = device_row(ahead_f, whole_f, f[4:], width)
    gath[0, ROWS : 2 * ROWS] = device_row(ahead_b, whole_b, g[4:], width)
    gath_copies = []
    for d in range(1, n_tm):
        copy = pltpu.make_async_remote_copy(
            src_ref=gath.at[0],
            dst_ref=gath.at[d],
            send_sem=gath_send.at[d],
            recv_sem=gath_recv.at[d],
            device_id={"tm": lax.rem(me + d, n_tm)},
            device_id_type=MESH,
        )
        copy.start()
        gath_copies.append(copy)

    for copy in read_sends:
        copy.wait()
    lane = lax.broadcasted_iota(jnp.int32, (outs, LANES), 1)
    for e in range(n_ch):
        slab = reads.at[(n_ch - e) % n_ch]
        for k in range(2):
            part = slab[pl.ds(k, outs, stride=2), :]
            for h in range(blocks):
                shift = lax.rem(h * width + LANES - group * width, LANES)
                moved = pltpu.roll(part, shift, 1)
                moved = jnp.where((lane >= h * width) & (lane < (h + 1) * width), moved, 0.0)
                high, low = split(moved)
                weights[e, 0, h * outs : (h + 1) * outs, k * LANES : (k + 1) * LANES] = high
                weights[e, 1, h * outs : (h + 1) * outs, k * LANES : (k + 1) * LANES] = low

    for copy in gath_copies:
        copy.wait()

    def along(order, base):
        zero = jnp.zeros((1, LANES), jnp.float32)
        cr, ci, keep_r, keep_i, norm = zero, zero, zero, zero, zero
        for j in order:
            stat = gath[lax.rem(me - j + n_tm, n_tm), base : base + ROWS]
            zr, zi, tr, ti, d0, d1r, d1i, d2 = [stat[i : i + 1] for i in range(ROWS)]
            mine = jnp.full((1, LANES), me, jnp.int32) == j
            keep_r = jnp.where(mine, cr, keep_r)
            keep_i = jnp.where(mine, ci, keep_i)
            norm = norm + (d0 + 2.0 * (cr * d1r + ci * d1i) + (cr * cr + ci * ci) * d2)
            cr, ci = zr * cr - zi * ci + tr, zr * ci + zi * cr + ti
        scale = 1.0 / jnp.sqrt(norm / (2.0 * steps * n_tm) + epsilon)
        return keep_r, keep_i, scale

    def carries(ahead, order, base):
        cr, ci, scale = along(order, base)
        pr, pi, ur, ui = ahead
        xr, xi = cmul(pr, pi, cr, ci)
        return (xr + ur) * scale, (xi + ui) * scale, jnp.broadcast_to(scale, (ROWS, LANES))

    cr, ci, cs = carries(ahead_f, range(n_tm), 0)
    dr, di, ds = carries(ahead_b, range(n_tm - 1, -1, -1), ROWS)

    def smooth_step(s, _):
        fr, fi, ar, ai, gr, gi, br, bi = [scans[i, s] for i in range(8)]
        rows = pl.ds(s, ROWS, stride=pitch)
        smooth.at[0][rows, :] = (fr * cs + (ar * cr - ai * ci)) + (gr * ds + (br * dr - bi * di))
        smooth.at[1][rows, :] = (fi * cs + (ar * ci + ai * cr)) + (gi * ds + (br * di + bi * dr))
        return 0

    lax.fori_loop(0, length, smooth_step, 0, unroll=4)

    def tile_of(b):
        per = LANES // length if length < LANES else 1
        first = b * LANES // length
        offset = b * LANES - first * length
        size = min(length, LANES)
        return [
            jnp.concatenate(
                [
                    smooth[c, (first + i) * pitch + offset : (first + i) * pitch + offset + size, :]
                    for i in range(per)
                ],
                axis=0,
            )
            for c in range(2)
        ]

    def product(e, right):
        high, low = right
        dims = (((1,), (1,)), ((), ()))
        dot = functools.partial(
            lax.dot_general, dimension_numbers=dims, preferred_element_type=jnp.float32
        )
        return dot(weights[e, 0], high) + (dot(weights[e, 1], high) + dot(weights[e, 0], low))

    part_copies = {}
    rights = []
    for b in range(tiles):
        right = split(jnp.concatenate(tile_of(b), axis=1))
        rights.append(right)
        for e in range(1, n_ch):
            sends[e - 1, b] = product(e, right)
            copy = pltpu.make_async_remote_copy(
                src_ref=sends.at[e - 1, b],
                dst_ref=recvs.at[e - 1, b],
                send_sem=part_send.at[e - 1, b],
                recv_sem=part_recv.at[e - 1, b],
                device_id={"chan": lax.rem(group + e, n_ch)},
                device_id_type=MESH,
            )
            copy.start()
            part_copies[e, b] = copy
    for b in range(tiles):
        right = split(jnp.concatenate(tile_of(b), axis=1))
        own[b] = product(0, right)
    out_copies = []
    for b in range(tiles):
        total = own[b]
        for e in range(1, n_ch):
            part_copies[e, b].wait_recv()
            total = total + recvs[e - 1, b]
        for h in range(blocks):
            at = h * span + b * LANES
            final[:, at : at + LANES] = total[h * outs : (h + 1) * outs]
            copy = pltpu.make_async_copy(
                final.at[:, at : at + LANES], out.at[:, at : at + LANES], out_sem.at[b, h]
            )
            copy.start()
            out_copies.append(copy)
    for copy in part_copies.values():
        copy.wait_send()
    for copy in out_copies:
        copy.wait()


def on_device(n_tm, n_ch, trans, drive, back_drive, readout):
    width, steps = trans.shape[1], trans.shape[2]
    outs = readout.shape[0]
    blocks = LANES // width
    span = steps // blocks
    length = span // ROWS
    pitch = length + ROWS
    tiles = span // LANES
    f32 = jnp.float32
    dma = pltpu.SemaphoreType.DMA
    any_space = pl.BlockSpec(memory_space=pl.ANY)
    return pl.pallas_call(
        functools.partial(body, n_tm, n_ch),
        out_shape=jax.ShapeDtypeStruct((outs, steps), f32),
        in_specs=[any_space] * 4,
        out_specs=any_space,
        scratch_shapes=[
            pltpu.VMEM((6, width, steps), f32),
            pltpu.VMEM((6, ROWS * pitch, LANES), f32),
            pltpu.VMEM((8, length, ROWS, LANES), f32),
            pltpu.VMEM((2, ROWS * pitch, LANES), f32),
            pltpu.VMEM((n_ch, 2 * outs, LANES), f32),
            pltpu.VMEM((n_ch, 2, blocks * outs, 2 * LANES), jnp.bfloat16),
            pltpu.VMEM((n_tm, 2 * ROWS, LANES), f32),
            pltpu.VMEM((n_ch - 1, tiles, blocks * outs, LANES), f32),
            pltpu.VMEM((n_ch - 1, tiles, blocks * outs, LANES), f32),
            pltpu.VMEM((tiles, blocks * outs, LANES), f32),
            pltpu.VMEM((outs, steps), f32),
            dma((6,)),
            dma,
            dma((n_ch,)),
            dma((n_ch,)),
            dma((n_tm,)),
            dma((n_tm,)),
            dma((n_ch - 1, tiles)),
            dma((n_ch - 1, tiles)),
            dma((tiles, blocks)),
        ],
        compiler_params=pltpu.CompilerParams(
            collective_id=0, has_side_effects=True, vmem_limit_bytes=48 * 1024 * 1024
        ),
    )(trans, drive, back_drive, readout.reshape(2 * outs, readout.shape[2]))


def solution(mesh):
    in_specs = (
        P(None, "chan", "tm"),
        P(None, "chan", "tm"),
        P(None, "chan", "tm"),
        P("chan", None, None),
    )
    return jax.shard_map(
        functools.partial(on_device, mesh.shape["tm"], mesh.shape["chan"]),
        mesh=mesh,
        in_specs=in_specs,
        out_specs=P("chan", "tm"),
        check_vma=False,
    )
```

time: 185 us -> 33.1 us (0.18)
  blocking collectives: 97.5 us -> 0 us
  Pallas kernels: 0 us -> 27.2 us
  other arithmetic: 25.4 us -> 0 us
  local copies, waits for them, and re-layouts: 26.6 us -> 5.67 us
  waiting for transfers between devices: 17.8 us -> 0 us
  between operations: 15 us -> 0.01 us
  matrix products: 2.04 us -> 0 us
    unnamed x1 -> x0, blocking collectives: 63.1 us -> none
    psum x1 -> x0, blocking collectives: 29.5 us -> none  [on_device(): lax.psum((jnp.sum(forward_states[0] * forward_states[0] + forward_states[...]
    pallas_call x0 -> x1, Pallas kernels: none -> 27.2 us  [on_device(): pl.pallas_call(functools.partial(body, n_tm, n_ch), out_shape=jax.ShapeDt...]
    add x58 -> x0, other arithmetic: 22 us -> none  [the longest x37 13.1 us: compose(): later[2] * earlier[4] + later[3] * earlier[5] + later[5]]
    slice x100 -> x0, local copies, waits for them, and re-layouts: 18.1 us -> none  [the longest x62 8.38 us: shifted_part(): return jnp.concatenate([array[:, offset:], filler], axis=1)]
    reduce_scatter x1 -> x0, waiting for transfers between devices: 17.8 us -> none  [on_device(): lax.psum_scatter(jnp.dot(flat, right, precision=lax.Precision.HIGHEST, pr...]
    all_gather x1 -> x0, blocking collectives: 4.93 us -> none  [on_device(): full_readout = lax.all_gather(readout, 'chan', axis=0, tiled=True)]
    reduce_sum x2 -> x0, other arithmetic: 3.17 us -> none  [the longest x1 2.7 us: on_device(): jnp.sum(backward_states[0] * backward_states[0] + backward_states[1] * ba...]
  transfers between devices with their start and end apart: 1 -> 0, of which waited for: 1 -> 0; matrix products, arithmetic and copies ran while one was open for 0% -> 0% of each run, Pallas kernels for 0% -> 0%
where the time goes in v1:
time: 33.1 us; the launch traced here: 32.8 us
  Pallas kernels  27.2 us (82%)
  local copies, waits for them, and re-layouts  5.67 us (17%)
    pallas_call x1, Pallas kernels, on_device(): pl.pallas_call(functools.partial(body, n_tm, n_ch), out_shape=jax.ShapeDt...  27.2 us
    unnamed x9, local copies, waits for them, and re-layouts  5.67 us

profile of v1, /device:TPU:0, one launch (start us, length us, event | category | flops | bytes accessed | tf_op | source)
XLA Modules:
  0.0 32.8 jit_solution(16409125661669074590)
XLA Ops:
  0.0 0.0 copy-start
  0.0 1.6 %copy-done = f32[4,64,2048]{2,1,0:T(8,128)S(1)} copy-done((f32[4,64,2048]{2,1,0:T(8,128)S(1)}, f32[4,64,2048]{2,1,0:T(8,128)}, u32[]{:S(2)}) %copy-start) | copy-done | bytes 2097176
  1.6 0.0 copy-start.1
  1.6 1.2 %copy-done.1 = f32[2,64,2048]{2,1,0:T(8,128)S(1)} copy-done((f32[2,64,2048]{2,1,0:T(8,128)S(1)}, f32[2,64,2048]{2,1,0:T(8,128)}, u32[]{:S(2)}) %copy-start.1) | copy-done | bytes 1048600
  2.8 0.0 copy-start.2
  2.8 1.2 %copy-done.2 = f32[2,64,2048]{2,1,0:T(8,128)S(1)} copy-done((f32[2,64,2048]{2,1,0:T(8,128)S(1)}, f32[2,64,2048]{2,1,0:T(8,128)}, u32[]{:S(2)}) %copy-start.2) | copy-done | bytes 1048600
  4.0 0.0 copy-start.3
  4.0 0.8 %copy-done.3 = f32[64,2,128]{2,1,0:T(2,128)S(1)} copy-done((f32[64,2,128]{2,1,0:T(2,128)S(1)}, f32[64,2,128]{2,1,0:T(2,128)}, u32[]{:S(2)}) %copy-start.3) | copy-done | bytes 65560
  4.9 27.2 %shard_map.46 = f32[64,2048]{1,0:T(8,128)S(1)} custom-call(f32[4,64,2048]{2,1,0:T(8,128)S(1)} %copy-done, f32[2,64,2048]{2,1,0:T(8,128)S(1)} %copy-done.1, f32[2,64,2048]{2,1,0:T(8,128)S(1)} %copy-done.2, f32[128,128]{1,0:T(8,128)S(1)} %bitcast.1), custom_call_target="tpu_custom_call" | custom-call | tf_op jit(solution)/shard_map/pallas_call | solution.py:353
  32.0 0.8 %copy.6 = f32[64,2048]{1,0:T(8,128)} copy(f32[64,2048]{1,0:T(8,128)S(1)} %shard_map.46) | data formatting | bytes 1048576
Async XLA Ops:
  0.0 1.6 %copy-start = (f32[4,64,2048]{2,1,0:T(8,128)S(1)}, f32[4,64,2048]{2,1,0:T(8,128)}, u32[]{:S(2)}) copy-start(f32[4,64,2048]{2,1,0:T(8,128)} %trans.1) | copy-start | bytes 6291460
  1.6 1.2 %copy-start.1 = (f32[2,64,2048]{2,1,0:T(8,128)S(1)}, f32[2,64,2048]{2,1,0:T(8,128)}, u32[]{:S(2)}) copy-start(f32[2,64,2048]{2,1,0:T(8,128)} %drive.1) | copy-start | bytes 3145732
  2.8 1.2 %copy-start.2 = (f32[2,64,2048]{2,1,0:T(8,128)S(1)}, f32[2,64,2048]{2,1,0:T(8,128)}, u32[]{:S(2)}) copy-start(f32[2,64,2048]{2,1,0:T(8,128)} %back.1) | copy-start | bytes 3145732
  4.0 0.8 %copy-start.3 = (f32[64,2,128]{2,1,0:T(2,128)S(1)}, f32[64,2,128]{2,1,0:T(2,128)}, u32[]{:S(2)}) copy-start(f32[64,2,128]{2,1,0:T(2,128)} %param.7) | copy-start | bytes 196612

commit v2 on v1

--- a/solution.py
+++ b/solution.py
@@ -140,6 +140,7 @@
             barrier, inc=1, device_id={"chan": lax.rem(group + d, n_ch)}, device_id_type=MESH
         )
 
+    read_sends = []
     for i, copy in enumerate(loads):
         copy.wait()
         for b in range(tiles):
@@ -156,7 +157,6 @@
 
     read_copy.wait()
     pl.semaphore_wait(barrier, n_tm + n_ch - 2)
-    read_sends = []
     for d in range(1, n_ch):
         copy = pltpu.make_async_remote_copy(
             src_ref=reads.at[0],
@@ -210,8 +210,10 @@
     f, g = lax.fori_loop(0, length, scan_step, (start, start), unroll=4)
     ahead_f, whole_f = chunk_prefix((f[2], f[3], f[0], f[1]), width, False)
     ahead_b, whole_b = chunk_prefix((g[2], g[3], g[0], g[1]), width, True)
-    gath[0, 0:ROWS] = device_row(ahead_f, whole_f, f[4:], width)
-    gath[0, ROWS : 2 * ROWS] = device_row(ahead_b, whole_b, g[4:], width)
+    row_f = device_row(ahead_f, whole_f, f[4:], width)
+    row_b = device_row(ahead_b, whole_b, g[4:], width)
+    low = lax.broadcasted_iota(jnp.int32, (ROWS, LANES), 1) < LANES // 2
+    gath[0] = jnp.where(low, row_f, row_b)
     gath_copies = []
     for d in range(1, n_tm):
         copy = pltpu.make_async_remote_copy(
@@ -236,35 +238,40 @@
                 shift = lax.rem(h * width + LANES - group * width, LANES)
                 moved = pltpu.roll(part, shift, 1)
                 moved = jnp.where((lane >= h * width) & (lane < (h + 1) * width), moved, 0.0)
-                high, low = split(moved)
-                weights[e, 0, h * outs : (h + 1) * outs, k * LANES : (k + 1) * LANES] = high
-                weights[e, 1, h * outs : (h + 1) * outs, k * LANES : (k + 1) * LANES] = low
+                head, tail = split(moved)
+                weights[e, 0, h * outs : (h + 1) * outs, k * LANES : (k + 1) * LANES] = head
+                weights[e, 1, h * outs : (h + 1) * outs, k * LANES : (k + 1) * LANES] = tail
 
     for copy in gath_copies:
         copy.wait()
 
-    def along(order, base):
-        zero = jnp.zeros((1, LANES), jnp.float32)
-        cr, ci, keep_r, keep_i, norm = zero, zero, zero, zero, zero
-        for j in order:
-            stat = gath[lax.rem(me - j + n_tm, n_tm), base : base + ROWS]
-            zr, zi, tr, ti, d0, d1r, d1i, d2 = [stat[i : i + 1] for i in range(ROWS)]
-            mine = jnp.full((1, LANES), me, jnp.int32) == j
-            keep_r = jnp.where(mine, cr, keep_r)
-            keep_i = jnp.where(mine, ci, keep_i)
-            norm = norm + (d0 + 2.0 * (cr * d1r + ci * d1i) + (cr * cr + ci * ci) * d2)
-            cr, ci = zr * cr - zi * ci + tr, zr * ci + zi * cr + ti
-        scale = 1.0 / jnp.sqrt(norm / (2.0 * steps * n_tm) + epsilon)
-        return keep_r, keep_i, scale
-
-    def carries(ahead, order, base):
-        cr, ci, scale = along(order, base)
+    zero = jnp.zeros((1, LANES), jnp.float32)
+    low_row = lax.broadcasted_iota(jnp.int32, (1, LANES), 1) < LANES // 2
+    place = jnp.where(low_row, me, n_tm - 1 - me)
+    xr, xi, keep_r, keep_i, norm = zero, zero, zero, zero, zero
+    for j in range(n_tm):
+        stat = jnp.where(
+            low,
+            gath[lax.rem(me - j + n_tm, n_tm)],
+            gath[lax.rem(me + j + 1, n_tm)],
+        )
+        zr, zi, tr, ti, d0, d1r, d1i, d2 = [stat[i : i + 1] for i in range(ROWS)]
+        keep_r = jnp.where(place == j, xr, keep_r)
+        keep_i = jnp.where(place == j, xi, keep_i)
+        norm = norm + (d0 + 2.0 * (xr * d1r + xi * d1i) + (xr * xr + xi * xi) * d2)
+        xr, xi = zr * xr - zi * xi + tr, zr * xi + zi * xr + ti
+    scale = 1.0 / jnp.sqrt(norm / (2.0 * steps * n_tm) + epsilon)
+    mine = [jnp.broadcast_to(a, (ROWS, LANES)) for a in (keep_r, keep_i, scale)]
+    moved = [pltpu.roll(a, LANES // 2, 1) for a in mine]
+
+    def carries(ahead, whole):
+        kr, ki, by = whole
         pr, pi, ur, ui = ahead
-        xr, xi = cmul(pr, pi, cr, ci)
-        return (xr + ur) * scale, (xi + ui) * scale, jnp.broadcast_to(scale, (ROWS, LANES))
-
-    cr, ci, cs = carries(ahead_f, range(n_tm), 0)
-    dr, di, ds = carries(ahead_b, range(n_tm - 1, -1, -1), ROWS)
+        kr, ki = cmul(pr, pi, kr, ki)
+        return (kr + ur) * by, (ki + ui) * by, by
+
+    cr, ci, cs = carries(ahead_f, [jnp.where(low, a, b) for a, b in zip(mine, moved)])
+    dr, di, ds = carries(ahead_b, [jnp.where(low, b, a) for a, b in zip(mine, moved)])
 
     def smooth_step(s, _):
         fr, fi, ar, ai, gr, gi, br, bi = [scans[i, s] for i in range(8)]
@@ -362,7 +369,7 @@
             pltpu.VMEM((2, ROWS * pitch, LANES), f32),
             pltpu.VMEM((n_ch, 2 * outs, LANES), f32),
             pltpu.VMEM((n_ch, 2, blocks * outs, 2 * LANES), jnp.bfloat16),
-            pltpu.VMEM((n_tm, 2 * ROWS, LANES), f32),
+            pltpu.VMEM((n_tm, ROWS, LANES), f32),
             pltpu.VMEM((n_ch - 1, tiles, blocks * outs, LANES), f32),
             pltpu.VMEM((n_ch - 1, tiles, blocks * outs, LANES), f32),
             pltpu.VMEM((tiles, blocks * outs, LANES), f32),
@@ -378,7 +385,7 @@
             dma((tiles, blocks)),
         ],
         compiler_params=pltpu.CompilerParams(
-            collective_id=0, has_side_effects=True, vmem_limit_bytes=48 * 1024 * 1024
+            collective_id=0, has_side_effects=True, vmem_limit_bytes=67043328
         ),
     )(trans, drive, back_drive, readout.reshape(2 * outs, readout.shape[2]))
 

time: 33.1 us -> 29.7 us (0.90)
  local copies, waits for them, and re-layouts: 5.67 us -> 1.87 us
  Pallas kernels: 27.2 us -> 27.7 us
    unnamed x9 -> x1, local copies, waits for them, and re-layouts: 5.67 us -> 1.87 us
    pallas_call x1, Pallas kernels: 27.2 us -> 27.7 us  [on_device(): pl.pallas_call(functools.partial(body, n_tm, n_ch), out_shape=jax.ShapeDt...]
where the time goes in v2:
time: 29.7 us; the launch traced here: 29.5 us
  Pallas kernels  27.7 us (93%)
  local copies, waits for them, and re-layouts  1.87 us (6%)
    pallas_call x1, Pallas kernels, on_device(): pl.pallas_call(functools.partial(body, n_tm, n_ch), out_shape=jax.ShapeDt...  27.7 us
    unnamed x1, local copies, waits for them, and re-layouts  1.87 us

profile of v2, /device:TPU:0, one launch (start us, length us, event | category | flops | bytes accessed | tf_op | source)
XLA Modules:
  0.0 29.5 jit_solution(12042260661286472153)
XLA Ops:
  0.0 27.7 %shard_map.46 = f32[64,2048]{1,0:T(8,128)} custom-call(f32[4,64,2048]{2,1,0:T(8,128)} %trans.1, f32[2,64,2048]{2,1,0:T(8,128)} %drive.1, f32[2,64,2048]{2,1,0:T(8,128)} %back.1, f32[128,128]{1,0:T(8,128)} %bitcast.1), custom_call_target="tpu_custom_call" | custom-call | tf_op jit(solution)/shard_map/pallas_call | solution.py:360
  27.7 1.9 %copy.6 = f32[64,2048]{1,0:T(8,128)} copy(f32[64,2048]{1,0:T(8,128)} %shard_map.46) | data formatting | bytes 1048576

commit v3 on v2

--- a/solution.py
+++ b/solution.py
@@ -94,14 +94,13 @@
     raw,
     turned,
     scans,
-    smooth,
+    rights,
     reads,
     weights,
     gath,
     sends,
     recvs,
     own,
-    final,
     in_sem,
     read_in,
     read_send,
@@ -110,7 +109,6 @@
     gath_recv,
     part_send,
     part_recv,
-    out_sem,
 ):
     width = trans.shape[1]
     steps = trans.shape[2]
@@ -202,8 +200,8 @@
             turned.at[5][rows, :],
         )
         for i in range(4):
-            scans[i, s] = f[i]
-            scans[4 + i, r] = g[i]
+            scans[i, pl.ds(pl.multiple_of(s * ROWS, ROWS), ROWS), :] = f[i]
+            scans[4 + i, pl.ds(pl.multiple_of(r * ROWS, ROWS), ROWS), :] = g[i]
         return f, g
 
     start = (nil, nil, one, nil, nil, nil, nil, nil)
@@ -273,33 +271,23 @@
     cr, ci, cs = carries(ahead_f, [jnp.where(low, a, b) for a, b in zip(mine, moved)])
     dr, di, ds = carries(ahead_b, [jnp.where(low, b, a) for a, b in zip(mine, moved)])
 
-    def smooth_step(s, _):
-        fr, fi, ar, ai, gr, gi, br, bi = [scans[i, s] for i in range(8)]
-        rows = pl.ds(s, ROWS, stride=pitch)
-        smooth.at[0][rows, :] = (fr * cs + (ar * cr - ai * ci)) + (gr * ds + (br * dr - bi * di))
-        smooth.at[1][rows, :] = (fi * cs + (ar * ci + ai * cr)) + (gi * ds + (br * di + bi * dr))
-        return 0
-
-    lax.fori_loop(0, length, smooth_step, 0, unroll=4)
-
     def tile_of(b):
-        per = LANES // length if length < LANES else 1
-        first = b * LANES // length
-        offset = b * LANES - first * length
         size = min(length, LANES)
-        return [
-            jnp.concatenate(
-                [
-                    smooth[c, (first + i) * pitch + offset : (first + i) * pitch + offset + size, :]
-                    for i in range(per)
-                ],
-                axis=0,
-            )
-            for c in range(2)
-        ]
-
-    def product(e, right):
-        high, low = right
+        firsts, seconds = [], []
+        for at in range(b * LANES, (b + 1) * LANES, size):
+            k, offset = at // length, at % length
+            rows = pl.ds(offset * ROWS + k, size, stride=ROWS)
+            fr, fi, ar, ai, gr, gi, br, bi = [scans.at[i][rows, :] for i in range(8)]
+            er, ei, es = cr[k : k + 1], ci[k : k + 1], cs[k : k + 1]
+            hr, hi, hs = dr[k : k + 1], di[k : k + 1], ds[k : k + 1]
+            firsts.append((fr * es + (ar * er - ai * ei)) + (gr * hs + (br * hr - bi * hi)))
+            seconds.append((fi * es + (ar * ei + ai * er)) + (gi * hs + (br * hi + bi * hr)))
+        return jnp.concatenate(
+            [jnp.concatenate(firsts, axis=0), jnp.concatenate(seconds, axis=0)], axis=1
+        )
+
+    def product(e, b):
+        high, low = rights[b, 0], rights[b, 1]
         dims = (((1,), (1,)), ((), ()))
         dot = functools.partial(
             lax.dot_general, dimension_numbers=dims, preferred_element_type=jnp.float32
@@ -307,12 +295,10 @@
         return dot(weights[e, 0], high) + (dot(weights[e, 1], high) + dot(weights[e, 0], low))
 
     part_copies = {}
-    rights = []
     for b in range(tiles):
-        right = split(jnp.concatenate(tile_of(b), axis=1))
-        rights.append(right)
+        rights[b, 0], rights[b, 1] = split(tile_of(b))
         for e in range(1, n_ch):
-            sends[e - 1, b] = product(e, right)
+            sends[e - 1, b] = product(e, b)
             copy = pltpu.make_async_remote_copy(
                 src_ref=sends.at[e - 1, b],
                 dst_ref=recvs.at[e - 1, b],
@@ -324,9 +310,7 @@
             copy.start()
             part_copies[e, b] = copy
     for b in range(tiles):
-        right = split(jnp.concatenate(tile_of(b), axis=1))
-        own[b] = product(0, right)
-    out_copies = []
+        own[b] = product(0, b)
     for b in range(tiles):
         total = own[b]
         for e in range(1, n_ch):
@@ -334,16 +318,9 @@
             total = total + recvs[e - 1, b]
         for h in range(blocks):
             at = h * span + b * LANES
-            final[:, at : at + LANES] = total[h * outs : (h + 1) * outs]
-            copy = pltpu.make_async_copy(
-                final.at[:, at : at + LANES], out.at[:, at : at + LANES], out_sem.at[b, h]
-            )
-            copy.start()
-            out_copies.append(copy)
+            out[:, at : at + LANES] = total[h * outs : (h + 1) * outs]
     for copy in part_copies.values():
         copy.wait_send()
-    for copy in out_copies:
-        copy.wait()
 
 
 def on_device(n_tm, n_ch, trans, drive, back_drive, readout):
@@ -356,24 +333,23 @@
     tiles = span // LANES
     f32 = jnp.float32
     dma = pltpu.SemaphoreType.DMA
-    any_space = pl.BlockSpec(memory_space=pl.ANY)
+    far = pl.BlockSpec(memory_space=pl.ANY)
     return pl.pallas_call(
         functools.partial(body, n_tm, n_ch),
-        out_shape=jax.ShapeDtypeStruct((outs, steps), f32),
-        in_specs=[any_space] * 4,
-        out_specs=any_space,
+        out_shape=pltpu.VMEM((outs, steps), f32),
+        in_specs=[far] * 4,
+        out_specs=pl.BlockSpec(memory_space=pltpu.VMEM),
         scratch_shapes=[
             pltpu.VMEM((6, width, steps), f32),
             pltpu.VMEM((6, ROWS * pitch, LANES), f32),
-            pltpu.VMEM((8, length, ROWS, LANES), f32),
-            pltpu.VMEM((2, ROWS * pitch, LANES), f32),
+            pltpu.VMEM((8, length * ROWS, LANES), f32),
+            pltpu.VMEM((tiles, 2, LANES, 2 * LANES), jnp.bfloat16),
             pltpu.VMEM((n_ch, 2 * outs, LANES), f32),
             pltpu.VMEM((n_ch, 2, blocks * outs, 2 * LANES), jnp.bfloat16),
             pltpu.VMEM((n_tm, ROWS, LANES), f32),
             pltpu.VMEM((n_ch - 1, tiles, blocks * outs, LANES), f32),
             pltpu.VMEM((n_ch - 1, tiles, blocks * outs, LANES), f32),
             pltpu.VMEM((tiles, blocks * outs, LANES), f32),
-            pltpu.VMEM((outs, steps), f32),
             dma((6,)),
             dma,
             dma((n_ch,)),
@@ -382,10 +358,9 @@
             dma((n_tm,)),
             dma((n_ch - 1, tiles)),
             dma((n_ch - 1, tiles)),
-            dma((tiles, blocks)),
         ],
         compiler_params=pltpu.CompilerParams(
-            collective_id=0, has_side_effects=True, vmem_limit_bytes=67043328
+            collective_id=0, has_side_effects=True, vmem_limit_bytes=67043328 - 4 * outs * steps
         ),
     )(trans, drive, back_drive, readout.reshape(2 * outs, readout.shape[2]))
 

time: 29.7 us -> 27.3 us (0.919)
  Pallas kernels: 27.7 us -> 26.4 us
  local copies, waits for them, and re-layouts: 1.87 us -> 0.8 us
    pallas_call x1, Pallas kernels: 27.7 us -> 26.4 us  [on_device(): pl.pallas_call(functools.partial(body, n_tm, n_ch), out_shape=pltpu.VMEM(...]
    unnamed x1, local copies, waits for them, and re-layouts: 1.87 us -> 0.8 us
where the time goes in v3:
time: 27.3 us; the launch traced here: 27.2 us
  Pallas kernels  26.4 us (97%)
  local copies, waits for them, and re-layouts  0.8 us (3%)
    pallas_call x1, Pallas kernels, on_device(): pl.pallas_call(functools.partial(body, n_tm, n_ch), out_shape=pltpu.VMEM(...  26.4 us
    unnamed x1, local copies, waits for them, and re-layouts  0.8 us

profile of v3, /device:TPU:0, one launch (start us, length us, event | category | flops | bytes accessed | tf_op | source)
XLA Modules:
  0.0 27.2 jit_solution(4326174004433136624)
XLA Ops:
  0.0 26.4 %shard_map.46 = f32[64,2048]{1,0:T(8,128)S(1)} custom-call(f32[4,64,2048]{2,1,0:T(8,128)} %trans.1, f32[2,64,2048]{2,1,0:T(8,128)} %drive.1, f32[2,64,2048]{2,1,0:T(8,128)} %back.1, f32[128,128]{1,0:T(8,128)} %bitcast.1), custom_call_target="tpu_custom_call" | custom-call | tf_op jit(solution)/shard_map/pallas_call | solution.py:337
  26.4 0.8 %copy.6 = f32[64,2048]{1,0:T(8,128)} copy(f32[64,2048]{1,0:T(8,128)S(1)} %shard_map.46) | data formatting | bytes 1048576

commit v4 on v3

--- a/solution.py
+++ b/solution.py
@@ -123,10 +123,10 @@
 
     planes = (trans.at[0], trans.at[2], drive.at[0], drive.at[1], back.at[0], back.at[1])
     loads = [pltpu.make_async_copy(src, raw.at[i], in_sem.at[i]) for i, src in enumerate(planes)]
+    read_copy = pltpu.make_async_copy(readout, reads.at[0], read_in)
+    read_copy.start()
     for copy in loads:
         copy.start()
-    read_copy = pltpu.make_async_copy(readout, reads.at[0], read_in)
-    read_copy.start()
 
     barrier = pltpu.get_barrier_semaphore()
     for d in range(1, n_tm):
@@ -213,7 +213,7 @@
     low = lax.broadcasted_iota(jnp.int32, (ROWS, LANES), 1) < LANES // 2
     gath[0] = jnp.where(low, row_f, row_b)
     gath_copies = []
-    for d in range(1, n_tm):
+    for d in sorted(range(1, n_tm), key=lambda d: -min(d, n_tm - d)):
         copy = pltpu.make_async_remote_copy(
             src_ref=gath.at[0],
             dst_ref=gath.at[d],
@@ -292,7 +292,9 @@
         dot = functools.partial(
             lax.dot_general, dimension_numbers=dims, preferred_element_type=jnp.float32
         )
-        return dot(weights[e, 0], high) + (dot(weights[e, 1], high) + dot(weights[e, 0], low))
+        both = dot(weights[e].reshape(-1, 2 * LANES), high)
+        count = blocks * outs
+        return both[:count] + (both[count:] + dot(weights[e, 0], low))
 
     part_copies = {}
     for b in range(tiles):

time: 27.3 us -> 27.4 us (level)
  no operation moved by 1% of the time
where the time goes in v4:
time: 27.4 us; the launch traced here: 27.3 us
  Pallas kernels  26.5 us (97%)
  local copies, waits for them, and re-layouts  0.8 us (3%)
    pallas_call x1, Pallas kernels, on_device(): pl.pallas_call(functools.partial(body, n_tm, n_ch), out_shape=pltpu.VMEM(...  26.5 us
    unnamed x1, local copies, waits for them, and re-layouts  0.8 us

profile of v4, /device:TPU:0, one launch (start us, length us, event | category | flops | bytes accessed | tf_op | source)
XLA Modules:
  0.0 27.3 jit_solution(13978755486707788188)
XLA Ops:
  0.0 26.5 %shard_map.46 = f32[64,2048]{1,0:T(8,128)S(1)} custom-call(f32[4,64,2048]{2,1,0:T(8,128)} %trans.1, f32[2,64,2048]{2,1,0:T(8,128)} %drive.1, f32[2,64,2048]{2,1,0:T(8,128)} %back.1, f32[128,128]{1,0:T(8,128)} %bitcast.1), custom_call_target="tpu_custom_call" | custom-call | tf_op jit(solution)/shard_map/pallas_call | solution.py:339
  26.5 0.8 %copy.6 = f32[64,2048]{1,0:T(8,128)} copy(f32[64,2048]{1,0:T(8,128)S(1)} %shard_map.46) | data formatting | bytes 1048576
